TPU v7x, 32 devices: a whole 2x2x4 slice. The times are simulated.
32 devices in a mesh: groups: 2 (over y), tensor: 4 (over z), dp: 2 (over x), kv: 2 (over core).
Axes of the slice: x: 2, y: 2, z: 4, core: 2. Of those that a mesh axis runs over, the one named last changes fastest.
Arguments:
- residual: bfloat16 [64, 16384], P(('groups', 'dp'), ('tensor', 'kv')), parts along dimension 0, may hold values from -10 to 10
- query: bfloat16 [64, 8192], P(('groups', 'dp'), ('tensor', 'kv')), parts along dimension 0, may hold values from -60 to 60
- new_pair: bfloat16 [2, 64, 4, 128], P(None, ('groups', 'dp')), parts along dimension 1, may hold values from -8 to 8
- kv_cache: bfloat16 [2, 64, 2048, 4, 128], P(None, ('groups', 'dp'), ('tensor', 'kv')), parts along dimension 1, may hold values from -4.5 to 4.5
- lengths: int32 [64], P(('groups', 'dp')), parts along dimension 0, may hold values from 2 to 2048
- out_weight: bfloat16 [8192, 16384], P(('tensor', 'kv')), may hold values from -0.09375 to 0.09375
- norm_gain: bfloat16 [16384], replicated, may hold values from 0.25 to 1.75
Outputs:
- residual_out: bfloat16 [64, 16384], P(('groups', 'dp'), ('tensor', 'kv')), parts along dimension 0
- mlp_input: bfloat16 [64, 16384], P(('groups', 'dp')), parts along dimension 0
There are 2 independent parts, one for each index of `groups`. A program takes and returns all parts, laid end to end along the dimension named above; an argument that names none is the same for every part. Nothing has to cross between parts.
Inputs may be any that keep to these rules, and one draw needn't show every extreme that they name: Positions below lengths[b] hold sequence b's cache; the others are ignored.
All inputs are finite; a program needn't handle non-finite values.
Results may differ from a plain program's by a relative error of at most 0.007.
Values may be sent and summed in bfloat16 or wider, within the bound.
A program may use at most 128 MiB of HBM per device.

v0:
```python
import math
import jax
import jax.numpy as jnp
from jax import lax
from jax.sharding import PartitionSpec as P

D = 16384
QH = 64
KVH = 4
HD = 128
floor_value = -1e30
epsilon = 1e-05


def on_device(residual, query, new_pair, kv_cache, lengths, out_weight, norm_gain):
    seqs = residual.shape[0]
    width = residual.shape[1]
    per_dev = query.shape[1] // HD
    group = QH // KVH
    scaling = 1.0 / math.sqrt(HD)
    mine = lax.axis_index(("tensor", "kv"))
    queries = lax.all_gather(query, ("tensor", "kv"), axis=1, tiled=True)
    grouped = queries.reshape(seqs, KVH, group, HD)
    span = kv_cache.shape[2]
    places = mine * span + jnp.arange(span, dtype=jnp.int32)
    live = (places[None, :] < lengths[:, None])[:, None, None, :]
    scores = (
        jnp.einsum("bgjd,bpgd->bgjp", grouped, kv_cache[0], preferred_element_type=jnp.float32)
        * scaling
    )
    scores = jnp.where(live, scores, floor_value)
    highest = jnp.max(scores, axis=3)
    weights = jnp.where(live, jnp.exp(scores - highest[..., None]), 0.0)
    totals = jnp.sum(weights, axis=3)
    accum = jnp.einsum("bgjp,bpgd->bgjd", weights, kv_cache[1], preferred_element_type=jnp.float32)
    highest = highest.reshape(seqs, QH)
    totals = totals.reshape(seqs, QH)
    accum = accum.reshape(seqs, QH, HD)
    arrived = (
        lax.all_to_all(highest[None], ("tensor", "kv"), split_axis=2, concat_axis=0, tiled=True),
        lax.all_to_all(totals[None], ("tensor", "kv"), split_axis=2, concat_axis=0, tiled=True),
        lax.all_to_all(accum[None], ("tensor", "kv"), split_axis=2, concat_axis=0, tiled=True),
    )
    best = jnp.max(arrived[0], axis=0)
    factor = jnp.exp(arrived[0] - best[None])
    totals = jnp.sum(arrived[1] * factor, axis=0)
    accum = jnp.sum(arrived[2] * factor[..., None], axis=0)
    highest = best
    own_query = query.reshape(seqs, per_dev, HD).astype(jnp.float32)
    head_ids = mine * per_dev + jnp.arange(per_dev, dtype=jnp.int32)
    selector = (head_ids[:, None] // group == jnp.arange(KVH, dtype=jnp.int32)[None, :]).astype(
        jnp.float32
    )
    fresh_pair = jnp.einsum("hg,sbgd->sbhd", selector, new_pair.astype(jnp.float32))
    fresh = jnp.sum(own_query * fresh_pair[0], axis=2) * scaling
    best = jnp.maximum(highest, fresh)
    old_factor = jnp.exp(highest - best)
    new_factor = jnp.exp(fresh - best)
    totals = totals * old_factor + new_factor
    accum = accum * old_factor[..., None] + new_factor[..., None] * fresh_pair[1]
    attended = (accum / totals[..., None]).astype(jnp.bfloat16).reshape(seqs, per_dev * HD)
    partial_value = jnp.dot(attended, out_weight, preferred_element_type=jnp.float32)
    gain_wide = norm_gain.astype(jnp.float32)
    share = lax.psum_scatter(partial_value, ("tensor", "kv"), scatter_dimension=1, tiled=True)
    stream = (residual.astype(jnp.float32) + share).astype(jnp.bfloat16)
    widened = stream.astype(jnp.float32)
    squares = lax.psum(jnp.sum(widened * widened, axis=1), ("tensor", "kv"))
    gain_mine = lax.dynamic_slice_in_dim(gain_wide, mine * width, width, 0)
    piece = (widened * lax.rsqrt(squares / D + epsilon)[:, None] * gain_mine[None, :]).astype(
        jnp.bfloat16
    )
    normed = lax.all_gather(piece, ("tensor", "kv"), axis=1, tiled=True)
    return (stream, normed)


def solution(mesh):
    placed = (
        P(("groups", "dp"), ("tensor", "kv")),
        P(("groups", "dp"), ("tensor", "kv")),
        P(None, ("groups", "dp"), None, None),
        P(None, ("groups", "dp"), ("tensor", "kv"), None, None),
        P(("groups", "dp")),
        P(("tensor", "kv"), None),
        P(),
    )
    return jax.shard_map(
        on_device,
        mesh=mesh,
        in_specs=placed,
        out_specs=(P(("groups", "dp"), ("tensor", "kv")), P(("groups", "dp"), None)),
        check_vma=False,
    )
```

profile of v0, /device:TPU:0, one launch (start us, length us, event | category | flops | bytes accessed | tf_op | source)
XLA Modules:
  0.0 155.4 jit_solution(17761867516999163748)
XLA Ops:
  7.2 0.0 copy-start
  7.2 0.0 copy-start.2
  7.2 0.0 copy-start.4
  7.2 7.0 %fusion.25 = (bf16[1,16,256,4,128]{4,3,2,1,0:T(4,128)(2,1)}, bf16[1,16,256,4,128]{4,3,2,1,0:T(4,128)(2,1)S(1)}) fusion(bf16[2,16,256,4,128]{4,3,2,1,0:T(4,128)(2,1)} %param.10), kind=kLoop, calls=%fused_computation.48 | loop fusion | bytes 16777216 | tf_op jit(solution)/shard_map/slice | solution.py:35
  14.2 0.0 copy-done.2
  14.2 15.9 %all_gather.6 = bf16[16,8192]{1,0:T(8,128)(2,1)S(1)} all-gather(bf16[16,1024]{1,0:T(8,128)(2,1)S(1)} %copy-done.2), channel_id=1, replica_groups=mesh['groups'=2,'tensor'=4,'dp'=2,'kv'=2] {'tensor','kv'}, dimensions={1}, use_global_device_ids=true | all-gather | bytes 294912 | tf_op jit(solution)/shard_map/all_gather | solution.py:22
  30.2 0.1 broadcast_compare_fusion
  30.3 1.3 fusion.26
  31.6 0.4 fusion.4
  32.0 0.1 copy.42
  32.1 0.6 broadcast.100
  32.6 0.7 reduce.1
  33.3 0.7 reshape.118
  34.0 4.7 %all-to-all-start.2 = ((f32[8,1,128]{2,1,0:T(1,128)}), f32[8,1,128]{2,1,0:T(1,128)S(1)}, u32[]{:S(2)}, u32[]{:S(2)}) async-start(f32[8,1,128]{2,1,0:T(1,128)} %reshape.118), calls=%async_computation.2 | async-start | bytes 8192 | tf_op jit(solution)/shard_map/all_to_all | solution.py:41
  38.7 0.1 copy.35
  38.8 0.7 reduce.3
  39.5 0.7 reshape.116
  40.2 4.1 %all-to-all-done.2 = f32[8,1,128]{2,1,0:T(1,128)S(1)} async-done(((f32[8,1,128]{2,1,0:T(1,128)}), f32[8,1,128]{2,1,0:T(1,128)S(1)}, u32[]{:S(2)}, u32[]{:S(2)}) %all-to-all-start.2) | async-done | bytes 4128 | tf_op jit(solution)/shard_map/all_to_all | solution.py:41
  44.2 3.3 %all-to-all-start.1 = ((f32[8,1,128]{2,1,0:T(1,128)}), f32[8,1,128]{2,1,0:T(1,128)S(1)}, u32[]{:S(2)}, u32[]{:S(2)}) async-start(f32[8,1,128]{2,1,0:T(1,128)} %reshape.116), calls=%async_computation.1 | async-start | bytes 8192 | tf_op jit(solution)/shard_map/all_to_all | solution.py:40
  47.5 2.9 %fusion = f32[16,4,16,128]{3,2,1,0:T(8,128)S(1)} fusion(bf16[1,16,256,4,128]{4,3,2,1,0:T(4,128)(2,1)} %get-tuple-element.9, f32[16,4,16,256]{3,2,1,0:T(8,128)S(1)} %get-tuple-element.12, f32[16,4,16]{2,1,0:T(4,128)S(1)} %get-tuple-element.11, pred[16,256]{1,0:T(8,128)(4,1)S(1)} %broadcast_compare_fusion), kind=kOutput, calls=%fused_computation.1 | convolution fusion | flops 67633152 | bytes 5775360 | tf_op jit(solution)/shard_map/bgjp,bpgd->bgjd/dot_general | solution.py:35
  50.4 1.1 copy.34
  51.5 1.5 all-to-all-done.1
  53.0 3.5 %all-to-all-start = ((f32[1,16,64,128]{3,1,0,2:T(8,128)}), f32[1,16,64,128]{3,1,0,2:T(8,128)S(1)}, u32[]{:S(2)}, u32[]{:S(2)}) async-start(f32[1,16,64,128]{3,1,0,2:T(8,128)} %copy.34), calls=%async_computation | async-start | bytes 1048576 | tf_op jit(solution)/shard_map/all_to_all | solution.py:42
  56.5 0.0 reduce-scatter.2.cloned.1.call-start
  56.6 0.2 convolution_bitcast_fusion
  56.9 0.1 fusion.14
  57.0 0.1 copy.36
  57.0 0.6 reduce.2
  57.7 0.1 reshape.119
  57.8 0.6 reduce.4
  58.4 0.1 reshape.117
  58.6 0.1 copy.38
  58.6 0.1 copy.40
  58.7 13.1 %all-to-all-done = f32[1,16,64,128]{3,1,0,2:T(8,128)S(1)} async-done(((f32[1,16,64,128]{3,1,0,2:T(8,128)}), f32[1,16,64,128]{3,1,0,2:T(8,128)S(1)}, u32[]{:S(2)}, u32[]{:S(2)}) %all-to-all-start) | async-done | bytes 524320 | tf_op jit(solution)/shard_map/all_to_all | solution.py:42
  71.9 0.2 multiply_reduce_fusion
  72.1 0.1 mul.110
  72.1 0.1 div.30
  72.2 0.0 copy-start.3
  72.2 13.9 %fusion.15 = f32[16,16384]{1,0:T(8,128)} fusion(bf16[1024,16384]{1,0:T(8,128)(2,1)} %param.12, f32[2,8,8,128]{3,2,1,0:T(8,128)S(1)} %bitcast.90, f32[2,8,8,128]{3,2,1,0:T(8,128)S(1)} %bitcast.88, f32[2,8,8,128]{3,2,1,0:T(8,128)S(1)} %bitcast.89, f32[16,8,128]{2,0,1:T(8,128)S(1)} %multiply_reduce_fusion, f32[16,8]{0,1:T(8,128)S(1)} %get-tuple-element.5), kind=kOutput, calls=%fused_computation.28 | convolution fusion | flops 536952832 | bytes 34865664 | tf_op jit(solution)/shard_map/dot_general | solution.py:62
  86.2 0.0 reduce-scatter.2.cloned.1.call-update
  86.2 0.7 dynamic-slice_convert_fusion
  86.9 31.0 %reduce-scatter.2.cloned.1.call-done = f32[16,2048]{1,0:T(8,128)} async-done(((f32[16,16384]{1,0:T(8,128)}), f32[16,2048]{1,0:T(8,128)}) %reduce-scatter.2.cloned.1.call-update) | async-done | bytes 131088 | tf_op jit(solution)/shard_map/reduce_scatter | solution.py:64
  117.9 1.0 fusion.8
  118.9 13.8 %psum.7 = f32[16]{0:T(128)S(1)} all-reduce(f32[16]{0:T(128)S(1)} %get-tuple-element.2), channel_id=1, replica_groups=mesh['groups'=2,'tensor'=4,'dp'=2,'kv'=2] {'tensor','kv'}, use_global_device_ids=true, to_apply=%region_8.9 | all-reduce | flops 16 | bytes 128 | tf_op jit(solution)/shard_map/psum | solution.py:67
  132.8 0.1 fusion.10
  132.9 14.9 %all_gather.7 = bf16[16,16384]{1,0:T(8,128)(2,1)S(1)} all-gather(bf16[16,2048]{1,0:T(8,128)(2,1)S(1)} %fusion.10), channel_id=1, replica_groups=mesh['groups'=2,'tensor'=4,'dp'=2,'kv'=2] {'tensor','kv'}, dimensions={1}, use_global_device_ids=true | all-gather | bytes 589824 | tf_op jit(solution)/shard_map/all_gather | solution.py:72
  147.8 0.8 copy.70
  148.6 0.0 copy-done.1
  (14 shorter events, 0.1 us)
Async XLA Ops:
  7.2 49.5 %copy-start = (bf16[2,16,4,128]{3,2,1,0:T(4,128)(2,1)S(1)}, bf16[2,16,4,128]{3,2,1,0:T(4,128)(2,1)}, u32[]{:S(2)}) copy-start(bf16[2,16,4,128]{3,2,1,0:T(4,128)(2,1)} %param.9) | copy-start | bytes 98308
  7.2 7.0 %copy-start.2 = (bf16[16,1024]{1,0:T(8,128)(2,1)S(1)}, bf16[16,1024]{1,0:T(8,128)(2,1)}, u32[]{:S(2)}) copy-start(bf16[16,1024]{1,0:T(8,128)(2,1)} %param.8) | copy-start | bytes 98308
  7.2 23.0 %copy-start.4 = (s32[16]{0:T(128)S(1)}, s32[16]{0:T(128)}, u32[]{:S(2)}) copy-start(s32[16]{0:T(128)} %param.11) | copy-start | bytes 196
  34.0 10.2 %all-to-all-start.2 = ((f32[8,1,128]{2,1,0:T(1,128)}), f32[8,1,128]{2,1,0:T(1,128)S(1)}, u32[]{:S(2)}, u32[]{:S(2)}) async-start(f32[8,1,128]{2,1,0:T(1,128)} %reshape.118), calls=%async_computation.2 | async-start | bytes 8192 | tf_op jit(solution)/shard_map/all_to_all | solution.py:41
  44.2 8.8 %all-to-all-start.1 = ((f32[8,1,128]{2,1,0:T(1,128)}), f32[8,1,128]{2,1,0:T(1,128)S(1)}, u32[]{:S(2)}, u32[]{:S(2)}) async-start(f32[8,1,128]{2,1,0:T(1,128)} %reshape.116), calls=%async_computation.1 | async-start | bytes 8192 | tf_op jit(solution)/shard_map/all_to_all | solution.py:40
  53.0 18.9 %all-to-all-start = ((f32[1,16,64,128]{3,1,0,2:T(8,128)}), f32[1,16,64,128]{3,1,0,2:T(8,128)S(1)}, u32[]{:S(2)}, u32[]{:S(2)}) async-start(f32[1,16,64,128]{3,1,0,2:T(8,128)} %copy.34), calls=%async_computation | async-start | bytes 1048576 | tf_op jit(solution)/shard_map/all_to_all | solution.py:42
  56.5 61.3 %reduce-scatter.2.cloned.1.call-start = ((), (), s32[]{:S(2)}) async-start(), calls=%async_computation.4 | async-start | bytes 1179648 | tf_op jit(solution)/shard_map/reduce_scatter | solution.py:64
  72.2 45.7 %copy-start.3 = (bf16[16,2048]{1,0:T(8,128)(2,1)S(1)}, bf16[16,2048]{1,0:T(8,128)(2,1)}, u32[]{:S(2)}) copy-start(bf16[16,2048]{1,0:T(8,128)(2,1)} %param.7) | copy-start | bytes 196612
  118.9 29.7 %copy-start.1 = (bf16[16,2048]{1,0:T(8,128)(2,1)}, bf16[16,2048]{1,0:T(8,128)(2,1)S(1)}, u32[]{:S(2)}) copy-start(bf16[16,2048]{1,0:T(8,128)(2,1)S(1)} %get-tuple-element.15) | copy-start | bytes 196612
Sparse Core Ops, SparseCore 0:
  86.3 31.5 reduce-scatter.1
where the time goes:
time: 156 us; the launch traced here: 155 us
  waiting for transfers between devices  49.7 us (32%)
  blocking collectives  44.7 us (29%)
  matrix products  18.3 us (12%)
  between operations  14.2 us (9%)
  local copies, waits for them, and re-layouts  11.7 us (8%)
  starting transfers between devices  11.5 us (7%)
  other arithmetic  5.32 us (3%)
    reduce_scatter x1, waiting for transfers between devices, on_device(): lax.psum_scatter(partial_value, ('tensor', 'kv'), scatter_dimension=1, ti...  31 us
    all_gather x1, blocking collectives, on_device(): queries = lax.all_gather(query, ('tensor', 'kv'), axis=1, tiled=True)  15.9 us
    all_gather x1, blocking collectives, on_device(): normed = lax.all_gather(piece, ('tensor', 'kv'), axis=1, tiled=True)  14.9 us
    dot_general x1, matrix products, on_device(): jnp.dot(attended, out_weight, preferred_element_type=jnp.float32)  13.9 us
    psum x1, blocking collectives, on_device(): squares = lax.psum(jnp.sum(widened * widened, axis=1), ('tensor', 'kv'))  13.8 us
    all_to_all x1, waiting for transfers between devices, on_device(): lax.all_to_all(accum[None], ('tensor', 'kv'), split_axis=2, concat_axis=0...  13.1 us
    slice x1, local copies, waits for them, and re-layouts, on_device(): kv_cache[1]  7.01 us
    all_to_all x1, starting transfers between devices, on_device(): lax.all_to_all(totals[None], ('tensor', 'kv'), split_axis=2, concat_axis=...  4.68 us
  transfers between devices with their start and end apart: 4, of which 4 were waited for; matrix products, arithmetic and copies ran while one was open for 5% of the time, Pallas kernels for 0%

commit v1 on v0

--- a/solution.py
+++ b/solution.py
@@ -10,6 +10,13 @@
 HD = 128
 floor_value = -1e30
 epsilon = 1e-05
+
+
+def trade_parts(array, name, split, join):
+    size = lax.axis_size(name)
+    blocks = jnp.stack(jnp.split(array, size, axis=split), axis=0)
+    blocks = lax.all_to_all(blocks, name, split_axis=0, concat_axis=0)
+    return jnp.concatenate(blocks, axis=join)
 
 
 def on_device(residual, query, new_pair, kv_cache, lengths, out_weight, norm_gain):
@@ -39,7 +46,7 @@
     arrived = (
         lax.all_to_all(highest[None], ("tensor", "kv"), split_axis=2, concat_axis=0, tiled=True),
         lax.all_to_all(totals[None], ("tensor", "kv"), split_axis=2, concat_axis=0, tiled=True),
-        lax.all_to_all(accum[None], ("tensor", "kv"), split_axis=2, concat_axis=0, tiled=True),
+        trade_parts(accum[None], ("tensor", "kv"), 2, 0),
     )
     best = jnp.max(arrived[0], axis=0)
     factor = jnp.exp(arrived[0] - best[None])

time: 156 us -> 161 us (1.032)
  local copies, waits for them, and re-layouts: 11.7 us -> 15.8 us
  starting transfers between devices: 11.5 us -> 13.3 us
    unnamed x18 -> x25, local copies, waits for them, and re-layouts: 3 us -> 7.46 us
    all_to_all x1, waiting for transfers between devices: 4.05 us -> 0.01 us  [on_device(): lax.all_to_all(totals[None], ('tensor', 'kv'), split_axis=2, concat_axis=...]
    all_to_all x1, waiting for transfers between devices: 1.5 us -> 4.94 us  [on_device(): lax.all_to_all(highest[None], ('tensor', 'kv'), split_axis=2, concat_axis...]
    all_to_all x1, starting transfers between devices: 3.26 us -> 5.1 us  [on_device(): lax.all_to_all(highest[None], ('tensor', 'kv'), split_axis=2, concat_axis...]
  transfers between devices with their start and end apart: 4 -> 4, of which waited for: 4 -> 3; matrix products, arithmetic and copies ran while one was open for 5% -> 8% of each run, Pallas kernels for 0% -> 0%
where the time goes in v1:
time: 161 us
  waiting for transfers between devices  48.8 us (30%)
  blocking collectives  44.7 us (28%)
  matrix products  18.3 us (11%)
  local copies, waits for them, and re-layouts  15.8 us (10%)
  between operations  14.3 us (9%)
  starting transfers between devices  13.3 us (8%)
  other arithmetic  5.44 us (3%)
    reduce_scatter x1, waiting for transfers between devices, on_device(): lax.psum_scatter(partial_value, ('tensor', 'kv'), scatter_dimension=1, ti...  31 us
    all_gather x1, blocking collectives, on_device(): queries = lax.all_gather(query, ('tensor', 'kv'), axis=1, tiled=True)  15.9 us
    all_gather x1, blocking collectives, on_device(): normed = lax.all_gather(piece, ('tensor', 'kv'), axis=1, tiled=True)  14.9 us
    dot_general x1, matrix products, on_device(): jnp.dot(attended, out_weight, preferred_element_type=jnp.float32)  13.9 us
    psum x1, blocking collectives, on_device(): squares = lax.psum(jnp.sum(widened * widened, axis=1), ('tensor', 'kv'))  13.8 us
    all_to_all x1, waiting for transfers between devices, trade_parts(): blocks = lax.all_to_all(blocks, name, split_axis=0, concat_axis=0)  12.9 us
    unnamed x25, local copies, waits for them, and re-layouts  7.46 us
    slice x1, local copies, waits for them, and re-layouts, on_device(): kv_cache[1]  7.01 us
  transfers between devices with their start and end apart: 4, of which 3 were waited for; matrix products, arithmetic and copies ran while one was open for 8% of the time, Pallas kernels for 0%

profile of v1, /device:TPU:0, one launch (start us, length us, event | category | flops | bytes accessed | tf_op | source)
XLA Modules:
  0.0 160.6 jit_solution(4873312676708682732)
XLA Ops:
  7.2 7.0 %fusion.34 = (bf16[1,16,256,4,128]{4,3,2,1,0:T(4,128)(2,1)}, bf16[1,16,256,4,128]{4,3,2,1,0:T(4,128)(2,1)S(1)}) fusion(bf16[2,16,256,4,128]{4,3,2,1,0:T(4,128)(2,1)} %param.10), kind=kLoop, calls=%fused_computation.65 | loop fusion | bytes 16777216 | tf_op jit(solution)/shard_map/slice | solution.py:42
  14.2 15.9 %all_gather.6 = bf16[16,8192]{1,0:T(8,128)(2,1)S(1)} all-gather(bf16[16,1024]{1,0:T(8,128)(2,1)S(1)} %copy-done.2), channel_id=1, replica_groups=mesh['groups'=2,'tensor'=4,'dp'=2,'kv'=2] {'tensor','kv'}, dimensions={1}, use_global_device_ids=true | all-gather | bytes 294912 | tf_op jit(solution)/shard_map/all_gather | solution.py:29
  30.2 0.1 broadcast_compare_fusion
  30.3 1.3 fusion.35
  31.6 0.4 fusion.4
  32.0 0.1 copy.35
  32.1 0.5 broadcast.100
  32.6 0.7 reduce.1
  33.3 0.7 reshape.122
  34.0 4.7 %all-to-all-start.2 = ((f32[8,1,128]{2,1,0:T(1,128)}), f32[8,1,128]{2,1,0:T(1,128)S(1)}, u32[]{:S(2)}, u32[]{:S(2)}) async-start(f32[8,1,128]{2,1,0:T(1,128)} %reshape.122), calls=%async_computation.2 | async-start | bytes 8192 | tf_op jit(solution)/shard_map/all_to_all | solution.py:48
  38.7 2.9 %fusion = f32[16,4,16,128]{3,2,1,0:T(8,128)S(1)} fusion(bf16[1,16,256,4,128]{4,3,2,1,0:T(4,128)(2,1)} %get-tuple-element.9, f32[16,4,16,256]{3,2,1,0:T(8,128)S(1)} %get-tuple-element.12, f32[16,4,16]{2,1,0:T(4,128)S(1)} %get-tuple-element.11, pred[16,256]{1,0:T(8,128)(4,1)S(1)} %broadcast_compare_fusion), kind=kOutput, calls=%fused_computation.1 | convolution fusion | flops 67633152 | bytes 5775360 | tf_op jit(solution)/shard_map/bgjp,bpgd->bgjd/dot_general | solution.py:42
  41.6 0.7 fusion.23
  42.2 0.6 fusion.22
  42.9 0.6 fusion.21
  43.5 0.6 fusion.20
  44.2 0.6 fusion.19
  44.8 0.6 fusion.18
  45.4 0.6 fusion.17
  46.1 0.1 copy.27
  46.1 0.7 reduce.3
  46.9 0.7 reshape.120
  47.5 5.1 %all-to-all-start.1 = ((f32[8,1,128]{2,1,0:T(1,128)}), f32[8,1,128]{2,1,0:T(1,128)S(1)}, u32[]{:S(2)}, u32[]{:S(2)}) async-start(f32[8,1,128]{2,1,0:T(1,128)} %reshape.120), calls=%async_computation.1 | async-start | bytes 8192 | tf_op jit(solution)/shard_map/all_to_all | solution.py:47
  52.6 0.6 fusion.16
  53.3 4.9 %all-to-all-done.1 = f32[8,1,128]{2,1,0:T(1,128)S(1)} async-done(((f32[8,1,128]{2,1,0:T(1,128)}), f32[8,1,128]{2,1,0:T(1,128)S(1)}, u32[]{:S(2)}, u32[]{:S(2)}) %all-to-all-start.1) | async-done | bytes 4128 | tf_op jit(solution)/shard_map/all_to_all | solution.py:47
  58.2 3.5 %all-to-all-start = ((f32[8,1,16,8,128]{4,3,2,1,0:T(8,128)}), f32[8,1,16,8,128]{4,3,2,1,0:T(8,128)S(1)}, u32[]{:S(2)}, u32[]{:S(2)}) async-start(f32[8,1,16,8,128]{4,3,2,1,0:T(8,128)} %fusion.16), calls=%async_computation | async-start | bytes 1048576 | tf_op jit(solution)/shard_map/all_to_all | solution.py:18
  61.8 0.2 convolution_bitcast_fusion
  62.1 0.1 fusion.15
  62.2 0.6 reduce.2
  62.9 0.1 reshape.123
  63.0 0.6 reduce.4
  63.6 0.1 reshape.121
  63.8 0.1 copy.28
  63.9 0.1 copy.30
  63.9 0.1 copy.31
  64.0 0.1 copy.33
  64.1 12.9 %all-to-all-done = f32[8,1,16,8,128]{4,3,2,1,0:T(8,128)S(1)} async-done(((f32[8,1,16,8,128]{4,3,2,1,0:T(8,128)}), f32[8,1,16,8,128]{4,3,2,1,0:T(8,128)S(1)}, u32[]{:S(2)}, u32[]{:S(2)}) %all-to-all-start) | async-done | bytes 524320 | tf_op jit(solution)/shard_map/all_to_all | solution.py:18
  77.0 0.2 fusion.5
  77.2 0.1 broadcast_multiply_fusion
  77.3 0.1 mul.110
  77.3 0.1 div.30
  77.4 13.9 %fusion.24 = f32[16,16384]{1,0:T(8,128)} fusion(bf16[1024,16384]{1,0:T(8,128)(2,1)} %param.12, f32[2,8,8,128]{3,2,1,0:T(8,128)S(1)} %bitcast.125, f32[2,8,8,128]{3,2,1,0:T(8,128)S(1)} %bitcast.122, f32[2,8,8,128]{3,2,1,0:T(8,128)S(1)} %bitcast.124, f32[2,8,8,128]{3,2,1,0:T(8,128)S(1)} %bitcast.123), kind=kOutput, calls=%fused_computation.44 | convolution fusion | flops 536936448 | bytes 34865152 | tf_op jit(solution)/shard_map/dot_general | solution.py:69
  91.4 0.7 dynamic-slice_convert_fusion
  92.1 31.0 %reduce-scatter.2.cloned.1.call-done = f32[16,2048]{1,0:T(8,128)} async-done(((f32[16,16384]{1,0:T(8,128)}), f32[16,2048]{1,0:T(8,128)}) %reduce-scatter.2.cloned.1.call-update) | async-done | bytes 131088 | tf_op jit(solution)/shard_map/reduce_scatter | solution.py:71
  123.0 1.0 fusion.9
  124.1 13.8 %psum.7 = f32[16]{0:T(128)S(1)} all-reduce(f32[16]{0:T(128)S(1)} %get-tuple-element.2), channel_id=1, replica_groups=mesh['groups'=2,'tensor'=4,'dp'=2,'kv'=2] {'tensor','kv'}, use_global_device_ids=true, to_apply=%region_8.9 | all-reduce | flops 16 | bytes 128 | tf_op jit(solution)/shard_map/psum | solution.py:74
  137.9 0.1 fusion.11
  138.0 14.9 %all_gather.7 = bf16[16,16384]{1,0:T(8,128)(2,1)S(1)} all-gather(bf16[16,2048]{1,0:T(8,128)(2,1)S(1)} %fusion.11), channel_id=1, replica_groups=mesh['groups'=2,'tensor'=4,'dp'=2,'kv'=2] {'tensor','kv'}, dimensions={1}, use_global_device_ids=true | all-gather | bytes 589824 | tf_op jit(solution)/shard_map/all_gather | solution.py:79
  152.9 0.8 copy.70
  (24 shorter events, 0.3 us)
Async XLA Ops:
  7.2 54.7 %copy-start = (bf16[2,16,4,128]{3,2,1,0:T(4,128)(2,1)S(1)}, bf16[2,16,4,128]{3,2,1,0:T(4,128)(2,1)}, u32[]{:S(2)}) copy-start(bf16[2,16,4,128]{3,2,1,0:T(4,128)(2,1)} %param.9) | copy-start | bytes 98308
  7.2 7.0 %copy-start.2 = (bf16[16,1024]{1,0:T(8,128)(2,1)S(1)}, bf16[16,1024]{1,0:T(8,128)(2,1)}, u32[]{:S(2)}) copy-start(bf16[16,1024]{1,0:T(8,128)(2,1)} %param.8) | copy-start | bytes 98308
  7.2 23.0 %copy-start.4 = (s32[16]{0:T(128)S(1)}, s32[16]{0:T(128)}, u32[]{:S(2)}) copy-start(s32[16]{0:T(128)} %param.11) | copy-start | bytes 196
  34.0 13.5 %all-to-all-start.2 = ((f32[8,1,128]{2,1,0:T(1,128)}), f32[8,1,128]{2,1,0:T(1,128)S(1)}, u32[]{:S(2)}, u32[]{:S(2)}) async-start(f32[8,1,128]{2,1,0:T(1,128)} %reshape.122), calls=%async_computation.2 | async-start | bytes 8192 | tf_op jit(solution)/shard_map/all_to_all | solution.py:48
  47.5 10.7 %all-to-all-start.1 = ((f32[8,1,128]{2,1,0:T(1,128)}), f32[8,1,128]{2,1,0:T(1,128)S(1)}, u32[]{:S(2)}, u32[]{:S(2)}) async-start(f32[8,1,128]{2,1,0:T(1,128)} %reshape.120), calls=%async_computation.1 | async-start | bytes 8192 | tf_op jit(solution)/shard_map/all_to_all | solution.py:47
  58.2 18.8 %all-to-all-start = ((f32[8,1,16,8,128]{4,3,2,1,0:T(8,128)}), f32[8,1,16,8,128]{4,3,2,1,0:T(8,128)S(1)}, u32[]{:S(2)}, u32[]{:S(2)}) async-start(f32[8,1,16,8,128]{4,3,2,1,0:T(8,128)} %fusion.16), calls=%async_computation | async-start | bytes 1048576 | tf_op jit(solution)/shard_map/all_to_all | solution.py:18
  61.7 61.3 %reduce-scatter.2.cloned.1.call-start = ((), (), s32[]{:S(2)}) async-start(), calls=%async_computation.4 | async-start | bytes 1179648 | tf_op jit(solution)/shard_map/reduce_scatter | solution.py:71
  77.4 45.6 %copy-start.3 = (bf16[16,2048]{1,0:T(8,128)(2,1)S(1)}, bf16[16,2048]{1,0:T(8,128)(2,1)}, u32[]{:S(2)}) copy-start(bf16[16,2048]{1,0:T(8,128)(2,1)} %param.7) | copy-start | bytes 196612
  124.1 29.7 %copy-start.1 = (bf16[16,2048]{1,0:T(8,128)(2,1)}, bf16[16,2048]{1,0:T(8,128)(2,1)S(1)}, u32[]{:S(2)}) copy-start(bf16[16,2048]{1,0:T(8,128)(2,1)S(1)} %get-tuple-element.15) | copy-start | bytes 196612
Sparse Core Ops, SparseCore 0:
  91.5 31.4 reduce-scatter.1
